TPU v7x, 32 devices: a whole 2x2x4 slice. The times are simulated.
32 devices in a mesh: pix: 32 (over z, y, x, core).
Axes of the slice: x: 2, y: 2, z: 4, core: 2. Of those that a mesh axis runs over, the one named last changes fastest.
Arguments:
- green: float32 [2048, 6144], P('pix'), may hold values from -200 to 200, as said below
- sketch: float32 [6144, 128], P('pix'), may hold values from -0.078125 to 0.078125
Outputs:
- basis: float32 [2048, 128], P('pix')
- projection: float32 [6144, 128], P('pix')
- spectrum_gram: float32 [128, 128], replicated
Inputs may be any that keep to these rules, and one draw needn't show every extreme that they name: `green`: finite real entries; each patch's column has its own scale.
All inputs are finite; a program needn't handle non-finite values.
Results may differ from a plain program's by a relative error of at most 0.000086.
Values sent between devices are 32-bit elements; how exact they have to be, the bound alone decides.
No kernel may reach another device: no remote copies, remote signals or barrier semaphores. Data moves between devices by JAX's collectives and lax.ppermute only.
A program may use at most 64 MiB of HBM per device.

v0:
```python
import jax
import jax.numpy as jnp
from jax import lax
from jax.sharding import PartitionSpec as P

PATCHES = 6144


def body(green, sketch):
    highest = lax.Precision.HIGHEST
    rows_here = green.shape[0]
    devices_pix = lax.axis_size("pix")
    total_pixels = rows_here * devices_pix
    columns = green
    sketched = jnp.dot(
        columns,
        lax.all_gather(sketch, "pix", axis=0, tiled=True),
        precision=highest,
        preferred_element_type=jnp.float32,
    )
    local_gram = jnp.dot(
        sketched.T, sketched, precision=highest, preferred_element_type=jnp.float32
    )
    columns = green
    raw_proj = lax.psum_scatter(
        lax.dot_general(
            columns,
            sketched,
            (((0,), (0,)), ((), ())),
            precision=highest,
            preferred_element_type=jnp.float32,
        ),
        "pix",
        scatter_dimension=0,
        tiled=True,
    )
    gram = lax.psum(local_gram, "pix")
    lower = jnp.linalg.cholesky(gram)
    orthonormal = jax.scipy.linalg.solve_triangular(lower, sketched.T, lower=True).T
    projection = jax.scipy.linalg.solve_triangular(lower, raw_proj.T, lower=True).T
    basis = jnp.sqrt(jnp.float32(total_pixels)) * orthonormal
    local_spec = jnp.dot(
        projection.T, projection, precision=highest, preferred_element_type=jnp.float32
    )
    spectrum_gram = lax.psum(local_spec, "pix") / jnp.float32(PATCHES)
    return (basis, projection, spectrum_gram)


def solution(mesh):
    in_specs = (P("pix", None), P("pix", None))
    out_specs = (P("pix", None), P("pix", None), P())
    return jax.shard_map(body, mesh=mesh, in_specs=in_specs, out_specs=out_specs, check_vma=False)
```

profile of v0, /device:TPU:1, one launch (start us, length us, event | category | flops | bytes accessed | tf_op | source)
XLA Modules:
  0.0 439.5 jit_solution(5103394524616839399)
XLA Ops:
  7.2 0.0 copy-start
  7.2 0.0 all-gather.2.cloned.1.call-start
  7.2 0.7 all-gather.2.cloned.1.call-update
  7.9 0.0 all-reduce.3.cloned.1.call-start
  8.0 64.5 %all-gather.2.cloned.1.call-done = f32[6144,128]{1,0:T(8,128)} async-done(((f32[192,128]{1,0:T(8,128)}), f32[6144,128]{1,0:T(8,128)}) %all-gather.2.cloned.1.call-update) | async-done | bytes 3145744 | tf_op jit(solution)/shard_map/all_gather | solution.py:17
  72.4 0.0 copy-done
  72.4 3.9 fusion.5
  76.3 0.9 fusion.6
  77.3 0.0 all-reduce.3.cloned.1.call-update
  77.3 0.0 reduce-scatter.4.cloned.1.call-start
  77.3 4.4 convolution_bitcast_fusion
  81.7 3.6 copy.10
  85.2 0.0 reduce-scatter.4.cloned.1.call-update
  85.3 0.2 all-reduce.5.cloned.1.call-start
  85.5 112.7 %all-reduce.3.cloned.1.call-done = f32[128,128]{0,1:T(8,128)} async-done(((f32[128,128]{0,1:T(8,128)}), f32[128,128]{0,1:T(8,128)}) %all-reduce.3.cloned.1.call-update) | async-done | bytes 65552 | tf_op jit(solution)/shard_map/psum | solution.py:37
  198.2 0.9 copy.8
  199.1 0.9 fusion.4
  200.0 11.7 %cholesky.16 = f32[128,128]{1,0:T(8,128)S(1)} custom-call(f32[128,128]{1,0:T(8,128)S(1)} %fusion.4), custom_call_target="Cholesky" | custom-call | tf_op jit(solution)/shard_map/jit(cholesky)/cholesky | solution.py:38
  211.7 0.6 compare_reduce_fusion
  212.4 0.7 fusion
  213.0 9.8 %custom-call.10 = f32[1,128,128]{1,2,0:T(8,128)S(1)} custom-call(f32[1,128,128]{2,1,0:T(8,128)S(1)} %fusion), custom_call_target="InvertDiagBlocksLowerTriangular" | custom-call | tf_op jit(solution)/shard_map/jit(_solve_triangular)/triangular_solve | solution.py:39
  222.9 80.8 %reduce-scatter.4.cloned.1.call-done = f32[192,128]{1,0:T(8,128)} async-done(((f32[6144,128]{1,0:T(8,128)}), f32[192,128]{1,0:T(8,128)}) %reduce-scatter.4.cloned.1.call-update) | async-done | bytes 98320
  303.6 1.1 fusion.1
  304.8 0.0 copy-start.1
  304.8 1.1 fusion.7
  305.9 0.0 all-reduce.5.cloned.1.call-update
  305.9 0.8 convolution_multiply_fusion
  306.7 124.8 %all-reduce.5.cloned.1.call-done = f32[128,128]{1,0:T(8,128)} async-done(((f32[128,128]{1,0:T(8,128)}), f32[128,128]{1,0:T(8,128)}) %all-reduce.5.cloned.1.call-update) | async-done | bytes 65552 | tf_op jit(solution)/shard_map/psum | solution.py:45
  431.5 1.5 broadcast_multiply_fusion
  433.0 0.0 copy-done.1
  (1 shorter events, 0.0 us)
Async XLA Ops:
  7.2 65.3 %copy-start = (f32[64,6144]{1,0:T(8,128)S(1)}, f32[64,6144]{1,0:T(8,128)}, u32[]{:S(2)}) copy-start(f32[64,6144]{1,0:T(8,128)} %param.2) | copy-start | bytes 4718596
  7.2 65.2 %all-gather.2.cloned.1.call-start = ((), (), s32[]{:S(2)}) async-start(), calls=%async_computation.1 | async-start | bytes 3244032 | tf_op jit(solution)/shard_map/all_gather | solution.py:17
  7.9 190.3 %all-reduce.3.cloned.1.call-start = ((), (), s32[]{:S(2)}) async-start(), calls=%async_computation.2 | async-start | bytes 131072 | tf_op jit(solution)/shard_map/psum | solution.py:37
  77.3 226.4 %reduce-scatter.4.cloned.1.call-start = ((), (), s32[]{:S(2)}) async-start(), calls=%async_computation.4 | async-start | bytes 3244032
  85.3 346.3 %all-reduce.5.cloned.1.call-start = ((), (), s32[]{:S(2)}) async-start(), calls=%async_computation.3 | async-start | bytes 131072 | tf_op jit(solution)/shard_map/psum | solution.py:45
  304.8 128.2 %copy-start.1 = (f32[128,192]{0,1:T(8,128)}, f32[128,192]{0,1:T(8,128)S(1)}, u32[]{:S(2)}) copy-start(f32[128,192]{0,1:T(8,128)S(1)} %fusion.1) | copy-start | bytes 294916
Sparse Core Ops, SparseCore 0:
  10.9 61.5 all-gather.1
  78.6 119.5 all-reduce.2
  203.6 99.9 reduce-scatter.3
  309.6 121.8 all-reduce.4
where the time goes:
time: 440 us
  waiting for transfers between devices  384 us (87%)
  other arithmetic  25.2 us (6%)
  between operations  13.8 us (3%)
  matrix products  12.2 us (3%)
  local copies, waits for them, and re-layouts  4.5 us (1%)
    psum x1, waiting for transfers between devices, body(): spectrum_gram = lax.psum(local_spec, 'pix') / jnp.float32(PATCHES)  125 us
    psum x1, waiting for transfers between devices, body(): gram = lax.psum(local_gram, 'pix')  113 us
    unnamed x5, waiting for transfers between devices  81.5 us
    all_gather x1, waiting for transfers between devices, body(): lax.all_gather(sketch, 'pix', axis=0, tiled=True)  64.5 us
    another operation x3, other arithmetic, body(): lower = jnp.linalg.cholesky(gram)  12.4 us
    another operation x2, other arithmetic, body(): jax.scipy.linalg.solve_triangular(lower, sketched.T, lower=True)  10.5 us
  transfers between devices with their start and end apart: 4, of which 4 were waited for; matrix products, arithmetic and copies ran while one was open for 8% of the time, Pallas kernels for 0%

commit v1 on v0

--- a/solution.py
+++ b/solution.py
@@ -34,7 +34,7 @@
         scatter_dimension=0,
         tiled=True,
     )
-    gram = lax.psum(local_gram, "pix")
+    gram = jnp.sum(lax.all_gather(local_gram, "pix"), axis=0)
     lower = jnp.linalg.cholesky(gram)
     orthonormal = jax.scipy.linalg.solve_triangular(lower, sketched.T, lower=True).T
     projection = jax.scipy.linalg.solve_triangular(lower, raw_proj.T, lower=True).T

time: 440 us -> 373 us (0.85)
  waiting for transfers between devices: 384 us -> 317 us
    psum x1 -> x0, waiting for transfers between devices: 113 us -> none  [body(): gram = lax.psum(local_gram, 'pix')]
    all_gather x0 -> x1, waiting for transfers between devices: none -> 46.8 us  [body(): gram = jnp.sum(lax.all_gather(local_gram, 'pix'), axis=0)]
  transfers between devices with their start and end apart: 4 -> 4, of which waited for: 4 -> 4; matrix products, arithmetic and copies ran while one was open for 8% -> 9% of each run, Pallas kernels for 0% -> 0%
where the time goes in v1:
time: 373 us
  waiting for transfers between devices  317 us (85%)
  other arithmetic  26 us (7%)
  between operations  13.8 us (4%)
  matrix products  12.2 us (3%)
    psum x1, waiting for transfers between devices, body(): spectrum_gram = lax.psum(local_spec, 'pix') / jnp.float32(PATCHES)  125 us
    unnamed x5, waiting for transfers between devices  80.6 us
    all_gather x1, waiting for transfers between devices, body(): lax.all_gather(sketch, 'pix', axis=0, tiled=True)  64.5 us
    all_gather x1, waiting for transfers between devices, body(): gram = jnp.sum(lax.all_gather(local_gram, 'pix'), axis=0)  46.8 us
    another operation x3, other arithmetic, body(): lower = jnp.linalg.cholesky(gram)  12.4 us
    another operation x2, other arithmetic, body(): jax.scipy.linalg.solve_triangular(lower, sketched.T, lower=True)  10.5 us
  transfers between devices with their start and end apart: 4, of which 4 were waited for; matrix products, arithmetic and copies ran while one was open for 9% of the time, Pallas kernels for 0%

profile of v1, /device:TPU:1, one launch (start us, length us, event | category | flops | bytes accessed | tf_op | source)
XLA Modules:
  0.0 372.9 jit_solution(11978824645821925223)
XLA Ops:
  7.2 0.0 copy-start
  7.2 0.0 all-gather.4.cloned.1.call-start
  7.2 0.7 all-gather.4.cloned.1.call-update
  7.9 0.0 all-gather.6.cloned.1.call-start
  8.0 64.5 %all-gather.4.cloned.1.call-done = f32[6144,128]{1,0:T(8,128)} async-done(((f32[192,128]{1,0:T(8,128)}), f32[6144,128]{1,0:T(8,128)}) %all-gather.4.cloned.1.call-update) | async-done | bytes 3145744 | tf_op jit(solution)/shard_map/all_gather | solution.py:17
  72.4 0.0 copy-done
  72.4 3.9 %fusion.5 = f32[64,128]{1,0:T(8,128)S(1)} fusion(f32[64,6144]{1,0:T(8,128)S(1)} %copy-done, f32[6144,128]{1,0:T(8,128)} %all-gather.4.cloned.1.call-done), kind=kOutput, calls=%fused_computation.14 | convolution fusion | flops 603979776 | bytes 4751360 | tf_op jit(solution)/shard_map/dot_general | solution.py:15
  76.3 0.9 fusion.6
  77.3 0.0 all-gather.6.cloned.1.call-update
  77.3 0.0 reduce-scatter.4.cloned.1.call-start
  77.3 4.4 %convolution_bitcast_fusion = f32[6144,128]{0,1:T(8,128)} fusion(f32[64,128]{1,0:T(8,128)S(1)} %fusion.5, f32[64,6144]{1,0:T(8,128)S(1)} %copy-done), kind=kOutput, calls=%fused_computation | convolution fusion | flops 603979776 | bytes 4751360 | tf_op jit(solution)/shard_map/dot_general | solution.py:26
  81.7 3.5 copy.7
  85.2 0.0 reduce-scatter.4.cloned.1.call-update
  85.3 0.2 all-reduce.2.cloned.1.call-start
  85.5 46.8 %all-gather.6.cloned.1.call-done = f32[4096,128]{1,0:T(8,128)} async-done(((f32[128,128]{1,0:T(8,128)}), f32[4096,128]{1,0:T(8,128)}) %all-gather.6.cloned.1.call-update) | async-done | bytes 2097168 | tf_op jit(solution)/shard_map/all_gather | solution.py:37
  132.3 1.7 reduce_sum.9
  134.0 0.1 copy.6
  134.2 11.7 %cholesky.16 = f32[128,128]{1,0:T(8,128)S(1)} custom-call(f32[128,128]{1,0:T(8,128)S(1)} %fusion.4), custom_call_target="Cholesky" | custom-call | tf_op jit(solution)/shard_map/jit(cholesky)/cholesky | solution.py:38
  145.9 0.6 compare_reduce_fusion
  146.5 0.7 fusion
  147.2 9.8 %custom-call.10 = f32[1,128,128]{1,2,0:T(8,128)S(1)} custom-call(f32[1,128,128]{2,1,0:T(8,128)S(1)} %fusion), custom_call_target="InvertDiagBlocksLowerTriangular" | custom-call | tf_op jit(solution)/shard_map/jit(_solve_triangular)/triangular_solve | solution.py:39
  157.0 79.9 %reduce-scatter.4.cloned.1.call-done = f32[192,128]{1,0:T(8,128)} async-done(((f32[6144,128]{1,0:T(8,128)}), f32[192,128]{1,0:T(8,128)}) %reduce-scatter.4.cloned.1.call-update) | async-done | bytes 98320
  236.9 1.1 fusion.1
  238.1 0.0 copy-start.1
  238.1 1.1 fusion.7
  239.1 0.0 all-reduce.2.cloned.1.call-update
  239.2 0.8 convolution_multiply_fusion
  240.0 125.0 %all-reduce.2.cloned.1.call-done = f32[128,128]{1,0:T(8,128)} async-done(((f32[128,128]{1,0:T(8,128)}), f32[128,128]{1,0:T(8,128)}) %all-reduce.2.cloned.1.call-update) | async-done | bytes 65552 | tf_op jit(solution)/shard_map/psum | solution.py:45
  364.9 1.5 broadcast_multiply_fusion
  366.4 0.0 copy-done.1
  (2 shorter events, 0.0 us)
Async XLA Ops:
  7.2 65.3 %copy-start = (f32[64,6144]{1,0:T(8,128)S(1)}, f32[64,6144]{1,0:T(8,128)}, u32[]{:S(2)}) copy-start(f32[64,6144]{1,0:T(8,128)} %param.2) | copy-start | bytes 4718596
  7.2 65.2 %all-gather.4.cloned.1.call-start = ((), (), s32[]{:S(2)}) async-start(), calls=%async_computation.1 | async-start | bytes 3244032 | tf_op jit(solution)/shard_map/all_gather | solution.py:17
  7.9 124.4 %all-gather.6.cloned.1.call-start = ((), (), s32[]{:S(2)}) async-start(), calls=%async_computation.3 | async-start | bytes 2162688 | tf_op jit(solution)/shard_map/all_gather | solution.py:37
  77.3 159.6 %reduce-scatter.4.cloned.1.call-start = ((), (), s32[]{:S(2)}) async-start(), calls=%async_computation.4 | async-start | bytes 3244032
  85.3 279.7 %all-reduce.2.cloned.1.call-start = ((), (), s32[]{:S(2)}) async-start(), calls=%async_computation.2 | async-start | bytes 131072 | tf_op jit(solution)/shard_map/psum | solution.py:45
  238.1 128.4 %copy-start.1 = (f32[128,192]{0,1:T(8,128)}, f32[128,192]{0,1:T(8,128)S(1)}, u32[]{:S(2)}) copy-start(f32[128,192]{0,1:T(8,128)S(1)} %fusion.1) | copy-start | bytes 294916
Sparse Core Ops, SparseCore 0:
  10.9 61.5 all-gather.3
  77.4 54.8 all-gather.5
  137.8 99.0 reduce-scatter.3
  242.9 121.9 all-reduce.1
